TPU v7x, 32 devices: a whole 2x2x4 slice. The times are simulated.
32 devices in a mesh: heads: 4 (over y, core), blk: 8 (over z, x).
Axes of the slice: x: 2, y: 2, z: 4, core: 2. Of those that a mesh axis runs over, the one named last changes fastest.
Arguments:
- tokens: bfloat16 [4096, 4096], P(('blk', 'heads')), may hold values from -6 to 6
- w_query: bfloat16 [4096, 2048], P('blk', 'heads'), may hold values from -0.75 to 0.75
- key_value_weight: bfloat16 [4096, 2, 512], P('blk', None, 'heads'), may hold values from -0.75 to 0.75
- w_out: bfloat16 [2048, 4096], P(('heads', 'blk')), may hold values from -0.5 to 0.5
- doc_lengths: int32 [16], replicated, may hold values from 1 to 1024, 4096 in all
Outputs:
- attended: bfloat16 [4096, 4096], P(('blk', 'heads'))
Inputs may be any that keep to these rules, and one draw needn't show every extreme that they name: `doc_lengths`: the 16 lengths sum to 4096; the longest document has exactly 1024 tokens.
All inputs are finite; a program needn't handle non-finite values.
Results may differ from a plain program's by a relative error of at most 0.012.
Values may be sent and summed in bfloat16 or wider, within the bound.
A program may use at most 128 MiB of HBM per device.

v0:
```python
import jax
import jax.numpy as jnp
from jax import lax
from jax.sharding import PartitionSpec as P

HEAD_SIZE = 128
norm_epsilon = 1e-05
rope_base = 500000.0
masked_score = -1e30


def shifted(value, axis, steps):
    count = lax.axis_size(axis)
    first, last = (max(0, -steps), min(count, count - steps))
    return lax.ppermute(value, axis, [(source, source + steps) for source in range(first, last)])


def locate_documents(positions, doc_lengths):
    ends = jnp.cumsum(doc_lengths)
    after = positions[:, None] >= ends[None, :]
    ident = jnp.sum(after.astype(jnp.int32), axis=1)
    starts = jnp.sum(jnp.where(after, doc_lengths[None, :], 0), axis=1)
    return (ident, starts)


def apply_rotation(values, relative_offset):
    half = values.shape[-1] // 2
    freqs = jnp.power(rope_base, -2.0 * jnp.arange(half, dtype=jnp.float32) / values.shape[-1])
    angle = relative_offset.astype(jnp.float32)[:, None] * freqs[None, :]
    cosine = jnp.cos(angle)[:, None, :]
    sine = jnp.sin(angle)[:, None, :]
    first = values[..., :half]
    second = values[..., half:]
    return jnp.concatenate(
        [first * cosine - second * sine, second * cosine + first * sine], axis=-1
    )


def on_device(tokens, w_query, key_value_weight, w_out, doc_lengths):
    blk_index = lax.axis_index("blk")
    reach = lax.axis_size("blk") // 4
    values = tokens.astype(jnp.float32)
    normalized_input = (
        values * lax.rsqrt(jnp.mean(values * values, axis=1, keepdims=True) + norm_epsilon)
    ).astype(jnp.bfloat16)
    block_input = lax.all_gather(normalized_input, "heads", axis=0, tiled=True)
    block_rows = block_input.shape[0]
    query_cols = w_query.shape[1]
    kv_cols = key_value_weight.shape[2]
    pieces = (
        lax.all_gather(w_query, "blk", axis=0, tiled=True),
        lax.all_gather(key_value_weight, "blk", axis=0, tiled=True),
    )
    count = pieces[0].shape[0]
    query_part = jnp.dot(block_input, pieces[0], preferred_element_type=jnp.float32)
    keyval_part = jnp.dot(
        block_input, pieces[1].reshape(count, 2 * kv_cols), preferred_element_type=jnp.float32
    )
    positions = blk_index * block_rows + jnp.arange(block_rows, dtype=jnp.int32)
    ident, starts = locate_documents(positions, doc_lengths)
    relative_offset = positions - starts
    query_heads = query_cols // HEAD_SIZE
    kv_heads = kv_cols // HEAD_SIZE
    head_group = query_heads // kv_heads
    query_rows = apply_rotation(
        query_part.reshape(block_rows, query_heads, HEAD_SIZE), relative_offset
    ).astype(jnp.bfloat16)
    query_rows = query_rows.reshape(block_rows, kv_heads, head_group, HEAD_SIZE)
    rotated_keys = apply_rotation(
        keyval_part[:, :kv_cols].reshape(block_rows, kv_heads, HEAD_SIZE), relative_offset
    ).astype(jnp.bfloat16)
    value_rows = (
        keyval_part[:, kv_cols:].reshape(block_rows, kv_heads, HEAD_SIZE).astype(jnp.bfloat16)
    )
    kv_block = jnp.stack([rotated_keys, value_rows], axis=1)
    scale = HEAD_SIZE ** (-0.5)

    def attend_tile(state, kv_now, distance):
        key_pos = (blk_index - distance) * block_rows + jnp.arange(block_rows, dtype=jnp.int32)
        key_doc, unused_k = locate_documents(key_pos, doc_lengths)
        keep = (
            (key_pos[None, :] >= 0)
            & (key_pos[None, :] <= positions[:, None])
            & (key_doc[None, :] == ident[:, None])
        )
        highest, totals, accum = state
        scores = (
            jnp.einsum(
                "qhgd,khd->hgqk", query_rows, kv_now[:, 0], preferred_element_type=jnp.float32
            )
            * scale
        )
        scores = jnp.where(keep, scores, masked_score)
        new_high = jnp.maximum(highest, jnp.max(scores, axis=-1))
        fading = jnp.exp(highest - new_high)
        probs = jnp.where(keep, jnp.exp(scores - new_high[..., None]), 0.0)
        totals = totals * fading + jnp.sum(probs, axis=-1)
        update = jnp.einsum(
            "hgqk,khd->hgqd",
            probs.astype(jnp.bfloat16),
            kv_now[:, 1],
            preferred_element_type=jnp.float32,
        )
        accum = accum * fading[..., None] + update
        return (new_high, totals, accum)

    initial = (
        jnp.full((kv_heads, head_group, block_rows), masked_score, jnp.float32),
        jnp.zeros((kv_heads, head_group, block_rows), jnp.float32),
        jnp.zeros((kv_heads, head_group, block_rows, HEAD_SIZE), jnp.float32),
    )
    state = attend_tile(initial, kv_block, 0)

    def advance(distance, carry):
        kv_now, inner = carry
        kv_now = shifted(kv_now, "blk", 1)
        return (kv_now, attend_tile(inner, kv_now, distance))

    unused_kv, state = lax.fori_loop(1, reach + 1, advance, (kv_block, state))
    highest, totals, accum = state
    mixed = accum / totals[..., None]
    mixed = mixed.transpose(2, 0, 1, 3).reshape(block_rows, query_cols).astype(jnp.bfloat16)
    head_rows = lax.all_gather(w_out, "blk", axis=0, tiled=True)
    return lax.psum_scatter(
        jnp.dot(mixed, head_rows, preferred_element_type=jnp.float32).astype(jnp.bfloat16),
        "heads",
        scatter_dimension=0,
        tiled=True,
    )


def solution(mesh):
    return jax.shard_map(
        on_device,
        mesh=mesh,
        in_specs=(
            P(("blk", "heads"), None),
            P("blk", "heads"),
            P("blk", None, "heads"),
            P(("heads", "blk"), None),
            P(),
        ),
        out_specs=P(("blk", "heads"), None),
        check_vma=False,
    )
```

profile of v0, /device:TPU:0, one launch (start us, length us, event | category | flops | bytes accessed | tf_op | source)
XLA Modules:
  0.0 311.8 jit_solution(1493680241664175790)
XLA Ops:
  7.3 1.5 fusion.24
  8.8 2.5 fusion.25
  13.0 1.0 multiply_cosine_fusion
  14.4 46.9 %all-gather.7.cloned.1.call-done = bf16[4096,2,128]{2,1,0:T(2,128)(2,1)} async-done(((bf16[512,2,128]{2,1,0:T(2,128)(2,1)}), bf16[4096,2,128]{2,1,0:T(2,128)(2,1)}) %all-gather.7.cloned.1.call-update) | async-done | bytes 2097168 | tf_op jit(solution)/shard_map/all_gather | solution.py:52
  61.3 34.6 %all-gather.5.cloned.1.call-done = bf16[512,4096]{1,0:T(8,128)(2,1)} async-done(((bf16[128,4096]{1,0:T(8,128)(2,1)}), bf16[512,4096]{1,0:T(8,128)(2,1)}) %all-gather.5.cloned.1.call-update) | async-done | bytes 4194320 | tf_op jit(solution)/shard_map/all_gather | solution.py:46
  95.9 4.2 %fusion.27 = f32[512,256]{0,1:T(8,128)S(1)} fusion(bf16[512,4096]{1,0:T(8,128)(2,1)} %all-gather.5.cloned.1.call-done, bf16[512,8,2,128]{3,2,1,0:T(2,128)(2,1)} %bitcast.161), kind=kOutput, calls=%fused_computation.38 | convolution fusion | flops 1073741824 | bytes 6815744 | tf_op jit(solution)/shard_map/dot_general | solution.py:56
  101.7 69.1 %all-gather.9.cloned.1.call-done = bf16[4096,512]{1,0:T(8,128)(2,1)} async-done(((bf16[512,512]{1,0:T(8,128)(2,1)}), bf16[4096,512]{1,0:T(8,128)(2,1)}) %all-gather.9.cloned.1.call-update) | async-done | bytes 4194320 | tf_op jit(solution)/shard_map/all_gather | solution.py:51
  170.8 5.8 %fusion.64 = f32[512,512]{0,1:T(8,128)S(1)} fusion(bf16[512,4096]{1,0:T(8,128)(2,1)} %all-gather.5.cloned.1.call-done, bf16[4096,512]{1,0:T(8,128)(2,1)} %all-gather.9.cloned.1.call-done), kind=kOutput, calls=%fused_computation.92 | convolution fusion | flops 2147483648 | bytes 9437184 | tf_op jit(solution)/shard_map/dot_general | solution.py:55
  178.1 1.2 fusion.21
  179.3 1.0 fusion.23
  180.4 1.6 fusion.36
  182.0 29.8 %while.22 = (s32[]{:T(128)}, bf16[512,2,1,128]{3,0,2,1:T(8,128)(2,1)S(1)}, f32[1,4,512]{2,1,0:T(4,128)S(1)}, f32[1,4,512]{2,1,0:T(4,128)S(1)}, f32[1,4,512,128]{...) while((s32[]{:T(128)}, ...), condition=%wide.region_10.11_spmd.clone, body=%wide.region_6.10_spmd.clone.sunk | while | flops 552107520 | bytes 18236672 | solution.py:119
  182.2 2.5 collective-permute-start
  185.1 6.1 %collective-permute-done = bf16[512,2,1,128]{3,0,2,1:T(8,128)(2,1)S(1)} collective-permute-done((bf16[512,2,1,128]{3,0,2,1:T(8,128)(2,1)S(1)}, bf16[512,2,1,128]{3,0,2,1:T(8,128)(2,1)S(1)}, u32[]{:S(2)}, u32[]{:S(2)}) %collective-permute-start) | collective-permute-done | bytes 262176 | tf_op jit(solution)/shard_map/while/body/eval_jaxpr/ppermute | solution.py:15
  192.1 1.0 fusion.78
  193.2 1.9 fusion.79
  195.2 8.8 %collective-permute-start = (bf16[512,2,1,128]{3,0,2,1:T(8,128)(2,1)S(1)}, bf16[512,2,1,128]{3,0,2,1:T(8,128)(2,1)S(1)}, u32[]{:S(2)}, u32[]{:S(2)}) collective-permute-start(bf16[512,2,1,128]{3,0,2,1:T(8,128)(2,1)S(1)} %get-tuple-element.431), channel_id=1, source_target_pairs={{0,1},{1,2},{2,3},{3,4},{4,5},{5,6},{6,7},{8,9},{9,10},{10,11},{11... | collective-permute-start | bytes 786440 | tf_op jit(solution)/shard_map/while/body/eval_jaxpr/ppermute | solution.py:15
  204.4 3.4 %collective-permute-done = bf16[512,2,1,128]{3,0,2,1:T(8,128)(2,1)S(1)} collective-permute-done((bf16[512,2,1,128]{3,0,2,1:T(8,128)(2,1)S(1)}, bf16[512,2,1,128]{3,0,2,1:T(8,128)(2,1)S(1)}, u32[]{:S(2)}, u32[]{:S(2)}) %collective-permute-start) | collective-permute-done | bytes 262176 | tf_op jit(solution)/shard_map/while/body/eval_jaxpr/ppermute | solution.py:15
  207.8 0.9 fusion.76
  208.7 1.0 fusion.78
  209.8 1.9 fusion.79
  212.2 41.3 %all-gather.11.cloned.1.call-done = bf16[512,4096]{1,0:T(8,128)(2,1)} async-done(((bf16[64,4096]{1,0:T(8,128)(2,1)}), bf16[512,4096]{1,0:T(8,128)(2,1)}) %all-gather.11.cloned.1.call-update) | async-done | bytes 4194320 | tf_op jit(solution)/shard_map/all_gather | solution.py:123
  253.6 6.5 %convolution_convert_fusion = bf16[512,4096]{1,0:T(8,128)(2,1)} fusion(bf16[512,512]{0,1:T(8,128)(2,1)S(1)} %bitcast.151, bf16[512,4096]{1,0:T(8,128)(2,1)} %all-gather.11.cloned.1.call-done), kind=kOutput, calls=%fused_computation.27 | convolution fusion | flops 2149580800 | bytes 8912896 | tf_op jit(solution)/shard_map/dot_general | solution.py:125
  260.1 45.2 %reduce-scatter.2.cloned.1.call-done = bf16[128,4096]{1,0:T(8,128)(2,1)} async-done(((bf16[512,4096]{1,0:T(8,128)(2,1)}), bf16[128,4096]{1,0:T(8,128)(2,1)}) %reduce-scatter.2.cloned.1.call-update) | async-done | bytes 1048592 | tf_op jit(solution)/shard_map/reduce_scatter | solution.py:124
  (57 shorter events, 8.1 us)
Async XLA Ops:
  6.5 6.2 %copy-start.3 = (s32[16]{0:T(128)S(1)}, s32[16]{0:T(128)}, u32[]{:S(2)}) copy-start(s32[16]{0:T(128)} %param.11) | copy-start | bytes 196
  6.5 54.8 %all-gather.7.cloned.1.call-start = ((), (), s32[]{:S(2)}) async-start(), calls=%async_computation.2 | async-start | bytes 2359296 | tf_op jit(solution)/shard_map/all_gather | solution.py:52
  7.3 88.6 %all-gather.5.cloned.1.call-start = ((), (), s32[]{:S(2)}) async-start(), calls=%async_computation.1 | async-start | bytes 5242880 | tf_op jit(solution)/shard_map/all_gather | solution.py:46
  11.3 159.5 %all-gather.9.cloned.1.call-start = ((), (), s32[]{:S(2)}) async-start(), calls=%async_computation.3 | async-start | bytes 4718592 | tf_op jit(solution)/shard_map/all_gather | solution.py:51
  12.1 241.5 %all-gather.11.cloned.1.call-start = ((), (), s32[]{:S(2)}) async-start(), calls=%async_computation.4 | async-start | bytes 4718592 | tf_op jit(solution)/shard_map/all_gather | solution.py:123
  12.6 292.7 %reduce-scatter.2.cloned.1.call-start = ((), (), s32[]{:S(2)}) async-start(), calls=%async_computation.5 | async-start | bytes 5242880 | tf_op jit(solution)/shard_map/reduce_scatter | solution.py:124
  100.0 0.8 copy-start
  178.1 2.3 copy-start.1
  180.4 1.6 copy-start.2
  182.2 9.1 %collective-permute-start = (bf16[512,2,1,128]{3,0,2,1:T(8,128)(2,1)S(1)}, bf16[512,2,1,128]{3,0,2,1:T(8,128)(2,1)S(1)}, u32[]{:S(2)}, u32[]{:S(2)}) collective-permute-start(bf16[512,2,1,128]{3,0,2,1:T(8,128)(2,1)S(1)} %get-tuple-element.431), channel_id=1, source_target_pairs={{0,1},{1,2},{2,3},{3,4},{4,5},{5,6},{6,7},{8,9},{9,10},{10,11},{11... | collective-permute-start | bytes 786440 | tf_op jit(solution)/shard_map/while/body/eval_jaxpr/ppermute | solution.py:15
  195.2 12.7 %collective-permute-start = (bf16[512,2,1,128]{3,0,2,1:T(8,128)(2,1)S(1)}, bf16[512,2,1,128]{3,0,2,1:T(8,128)(2,1)S(1)}, u32[]{:S(2)}, u32[]{:S(2)}) collective-permute-start(bf16[512,2,1,128]{3,0,2,1:T(8,128)(2,1)S(1)} %get-tuple-element.431), channel_id=1, source_target_pairs={{0,1},{1,2},{2,3},{3,4},{4,5},{5,6},{6,7},{8,9},{9,10},{10,11},{11... | collective-permute-start | bytes 786440 | tf_op jit(solution)/shard_map/while/body/eval_jaxpr/ppermute | solution.py:15
Sparse Core Ops, SparseCore 0:
  9.5 51.7 all-gather.6
  62.9 32.9 all-gather.4
  98.0 72.7 all-gather.8
  172.8 80.7 all-gather.10
  260.2 45.0 reduce-scatter.1
where the time goes:
time: 312 us
  waiting for transfers between devices  249 us (80%)
  matrix products  24.9 us (8%)
  between operations  13.3 us (4%)
  starting transfers between devices  11.4 us (4%)
  other arithmetic  11 us (4%)
    all_gather x1, waiting for transfers between devices, on_device(): lax.all_gather(w_query, 'blk', axis=0, tiled=True)  69.1 us
    all_gather x1, waiting for transfers between devices, on_device(): lax.all_gather(key_value_weight, 'blk', axis=0, tiled=True)  46.9 us
    reduce_scatter x1, waiting for transfers between devices, on_device(): lax.psum_scatter(jnp.dot(mixed, head_rows, preferred_element_type=jnp.flo...  45.2 us
    all_gather x1, waiting for transfers between devices, on_device(): head_rows = lax.all_gather(w_out, 'blk', axis=0, tiled=True)  41.3 us
    all_gather x1, waiting for transfers between devices, on_device(): block_input = lax.all_gather(normalized_input, 'heads', axis=0, tiled=True)  34.6 us
    ppermute x2, starting transfers between devices, shifted(): lax.ppermute(value, axis, [(source, source + steps) for source in range(f...  11.3 us
    ppermute x2, waiting for transfers between devices, shifted(): lax.ppermute(value, axis, [(source, source + steps) for source in range(f...  9.5 us
    dot_general x1, matrix products, on_device(): jnp.dot(mixed, head_rows, preferred_element_type=jnp.float32)  6.52 us
  transfers between devices with their start and end apart: 7, of which 7 were waited for; matrix products, arithmetic and copies ran while one was open for 10% of the time, Pallas kernels for 0%

commit v1 on v0

--- a/solution.py
+++ b/solution.py
@@ -49,7 +49,10 @@
     kv_cols = key_value_weight.shape[2]
     pieces = (
         lax.all_gather(w_query, "blk", axis=0, tiled=True),
-        lax.all_gather(key_value_weight, "blk", axis=0, tiled=True),
+        jnp.concatenate(
+            lax.all_to_all(jnp.stack([key_value_weight] * lax.axis_size("blk")), "blk", 0, 0),
+            axis=0,
+        ),
     )
     count = pieces[0].shape[0]
     query_part = jnp.dot(block_input, pieces[0], preferred_element_type=jnp.float32)

time: 312 us -> 271 us (0.87)
  waiting for transfers between devices: 249 us -> 199 us
  starting transfers between devices: 11.4 us -> 18.5 us
    all_to_all x0 -> x1, waiting for transfers between devices: none -> 62.6 us  [on_device(): lax.all_to_all(jnp.stack([key_value_weight] * lax.axis_size('blk')), 'blk...]
    all_gather x1 -> x0, waiting for transfers between devices: 46.9 us -> none  [on_device(): lax.all_gather(key_value_weight, 'blk', axis=0, tiled=True)]
    all_gather x1, waiting for transfers between devices: 34.6 us -> 0.01 us  [on_device(): block_input = lax.all_gather(normalized_input, 'heads', axis=0, tiled=True)]
    all_gather x1, waiting for transfers between devices: 69.1 us -> 38.8 us  [on_device(): lax.all_gather(w_query, 'blk', axis=0, tiled=True)]
    all_to_all x0 -> x1, starting transfers between devices: none -> 7.28 us  [on_device(): lax.all_to_all(jnp.stack([key_value_weight] * lax.axis_size('blk')), 'blk...]
  transfers between devices with their start and end apart: 7 -> 7, of which waited for: 7 -> 6; matrix products, arithmetic and copies ran while one was open for 10% -> 11% of each run, Pallas kernels for 0% -> 0%
where the time goes in v1:
time: 271 us
  waiting for transfers between devices  199 us (73%)
  matrix products  24.2 us (9%)
  starting transfers between devices  18.5 us (7%)
  between operations  13.3 us (5%)
  other arithmetic  11.1 us (4%)
  local copies, waits for them, and re-layouts  4.64 us (2%)
    all_to_all x1, waiting for transfers between devices, on_device(): lax.all_to_all(jnp.stack([key_value_weight] * lax.axis_size('blk')), 'blk...  62.6 us
    reduce_scatter x1, waiting for transfers between devices, on_device(): lax.psum_scatter(jnp.dot(mixed, head_rows, preferred_element_type=jnp.flo...  45.1 us
    all_gather x1, waiting for transfers between devices, on_device(): head_rows = lax.all_gather(w_out, 'blk', axis=0, tiled=True)  41.4 us
    all_gather x1, waiting for transfers between devices, on_device(): lax.all_gather(w_query, 'blk', axis=0, tiled=True)  38.8 us
    ppermute x2, starting transfers between devices, shifted(): lax.ppermute(value, axis, [(source, source + steps) for source in range(f...  11.1 us
    ppermute x2, waiting for transfers between devices, shifted(): lax.ppermute(value, axis, [(source, source + steps) for source in range(f...  9.66 us
    all_to_all x1, starting transfers between devices, on_device(): lax.all_to_all(jnp.stack([key_value_weight] * lax.axis_size('blk')), 'blk...  7.28 us
    dot_general x1, matrix products, on_device(): jnp.dot(mixed, head_rows, preferred_element_type=jnp.float32)  6.52 us
  transfers between devices with their start and end apart: 7, of which 6 were waited for; matrix products, arithmetic and copies ran while one was open for 11% of the time, Pallas kernels for 0%

profile of v1, /device:TPU:0, one launch (start us, length us, event | category | flops | bytes accessed | tf_op | source)
XLA Modules:
  0.0 271.1 jit_solution(4300637683087617391)
XLA Ops:
  6.5 1.6 fusion.24
  8.1 2.5 fusion.25
  11.4 2.4 stack.6
  13.8 7.3 %all-to-all-start = ((bf16[8,512,2,128]{3,2,1,0:T(2,128)(2,1)}), bf16[8,512,2,128]{3,2,1,0:T(2,128)(2,1)S(1)}, u32[]{:S(2)}, u32[]{:S(2)}) async-start(bf16[8,512,2,128]{3,2,1,0:T(2,128)(2,1)} %stack.6), calls=%async_computation | async-start | bytes 4194304 | tf_op jit(solution)/shard_map/all_to_all | solution.py:53
  22.5 1.0 multiply_cosine_fusion
  23.5 62.6 %all-to-all-done = bf16[8,512,2,128]{3,2,1,0:T(2,128)(2,1)S(1)} async-done(((bf16[8,512,2,128]{3,2,1,0:T(2,128)(2,1)}), bf16[8,512,2,128]{3,2,1,0:T(2,128)(2,1)S(1)}, u32[]{:S(2)}, u32[]{:S(2)}) %all-to-all-start) | async-done | bytes 2097184 | tf_op jit(solution)/shard_map/all_to_all | solution.py:53
  86.2 3.5 %fusion.27 = f32[512,256]{0,1:T(8,128)S(1)} fusion(bf16[512,4096]{1,0:T(8,128)(2,1)} %all-gather.4.cloned.1.call-done, bf16[512,8,2,128]{3,2,1,0:T(2,128)(2,1)S(1)} %bitcast.153), kind=kOutput, calls=%fused_computation.38 | convolution fusion | flops 1073741824 | bytes 6815744 | tf_op jit(solution)/shard_map/dot_general | solution.py:59
  91.3 38.8 %all-gather.6.cloned.1.call-done = bf16[4096,512]{1,0:T(8,128)(2,1)} async-done(((bf16[512,512]{1,0:T(8,128)(2,1)}), bf16[4096,512]{1,0:T(8,128)(2,1)}) %all-gather.6.cloned.1.call-update) | async-done | bytes 4194320 | tf_op jit(solution)/shard_map/all_gather | solution.py:51
  130.1 5.8 %fusion.64 = f32[512,512]{0,1:T(8,128)S(1)} fusion(bf16[512,4096]{1,0:T(8,128)(2,1)} %all-gather.4.cloned.1.call-done, bf16[4096,512]{1,0:T(8,128)(2,1)} %all-gather.6.cloned.1.call-done), kind=kOutput, calls=%fused_computation.92 | convolution fusion | flops 2147483648 | bytes 9437184 | tf_op jit(solution)/shard_map/dot_general | solution.py:58
  137.4 1.2 fusion.21
  138.6 1.0 fusion.23
  139.7 1.6 fusion.36
  141.3 29.8 %while.22 = (s32[]{:T(128)}, bf16[512,2,1,128]{3,0,2,1:T(8,128)(2,1)S(1)}, f32[1,4,512]{2,1,0:T(4,128)S(1)}, f32[1,4,512]{2,1,0:T(4,128)S(1)}, f32[1,4,512,128]{...) while((s32[]{:T(128)}, ...), condition=%wide.region_10.11_spmd.clone, body=%wide.region_6.10_spmd.clone.sunk | while | flops 552107520 | bytes 18236672 | solution.py:122
  141.5 2.5 collective-permute-start
  144.4 6.3 %collective-permute-done = bf16[512,2,1,128]{3,0,2,1:T(8,128)(2,1)S(1)} collective-permute-done((bf16[512,2,1,128]{3,0,2,1:T(8,128)(2,1)S(1)}, bf16[512,2,1,128]{3,0,2,1:T(8,128)(2,1)S(1)}, u32[]{:S(2)}, u32[]{:S(2)}) %collective-permute-start) | collective-permute-done | bytes 262176 | tf_op jit(solution)/shard_map/while/body/eval_jaxpr/ppermute | solution.py:15
  151.6 1.0 fusion.78
  152.7 1.9 fusion.79
  154.6 8.6 %collective-permute-start = (bf16[512,2,1,128]{3,0,2,1:T(8,128)(2,1)S(1)}, bf16[512,2,1,128]{3,0,2,1:T(8,128)(2,1)S(1)}, u32[]{:S(2)}, u32[]{:S(2)}) collective-permute-start(bf16[512,2,1,128]{3,0,2,1:T(8,128)(2,1)S(1)} %get-tuple-element.421), channel_id=1, source_target_pairs={{0,1},{1,2},{2,3},{3,4},{4,5},{5,6},{6,7},{8,9},{9,10},{10,11},{11... | collective-permute-start | bytes 786440 | tf_op jit(solution)/shard_map/while/body/eval_jaxpr/ppermute | solution.py:15
  163.7 3.4 %collective-permute-done = bf16[512,2,1,128]{3,0,2,1:T(8,128)(2,1)S(1)} collective-permute-done((bf16[512,2,1,128]{3,0,2,1:T(8,128)(2,1)S(1)}, bf16[512,2,1,128]{3,0,2,1:T(8,128)(2,1)S(1)}, u32[]{:S(2)}, u32[]{:S(2)}) %collective-permute-start) | collective-permute-done | bytes 262176 | tf_op jit(solution)/shard_map/while/body/eval_jaxpr/ppermute | solution.py:15
  168.0 1.0 fusion.78
  169.1 1.9 fusion.79
  171.5 41.4 %all-gather.8.cloned.1.call-done = bf16[512,4096]{1,0:T(8,128)(2,1)} async-done(((bf16[64,4096]{1,0:T(8,128)(2,1)}), bf16[512,4096]{1,0:T(8,128)(2,1)}) %all-gather.8.cloned.1.call-update) | async-done | bytes 4194320 | tf_op jit(solution)/shard_map/all_gather | solution.py:126
  212.9 6.5 %convolution_convert_fusion = bf16[512,4096]{1,0:T(8,128)(2,1)} fusion(bf16[512,512]{0,1:T(8,128)(2,1)S(1)} %bitcast.152, bf16[512,4096]{1,0:T(8,128)(2,1)} %all-gather.8.cloned.1.call-done), kind=kOutput, calls=%fused_computation.27 | convolution fusion | flops 2149580800 | bytes 8912896 | tf_op jit(solution)/shard_map/dot_general | solution.py:128
  219.5 45.1 %reduce-scatter.2.cloned.1.call-done = bf16[128,4096]{1,0:T(8,128)(2,1)} async-done(((bf16[512,4096]{1,0:T(8,128)(2,1)}), bf16[128,4096]{1,0:T(8,128)(2,1)}) %reduce-scatter.2.cloned.1.call-update) | async-done | bytes 1048592 | tf_op jit(solution)/shard_map/reduce_scatter | solution.py:127
  (59 shorter events, 8.4 us)
Async XLA Ops:
  6.5 4.8 %copy-start.2 = (bf16[512,2,128]{2,1,0:T(2,128)(2,1)S(1)}, bf16[512,2,128]{2,1,0:T(2,128)(2,1)}, u32[]{:S(2)}) copy-start(bf16[512,2,128]{2,1,0:T(2,128)(2,1)} %param.9) | copy-start | bytes 786436
  6.5 79.6 %all-gather.4.cloned.1.call-start = ((), (), s32[]{:S(2)}) async-start(), calls=%async_computation.2 | async-start | bytes 5242880 | tf_op jit(solution)/shard_map/all_gather | solution.py:46
  10.6 11.3 %copy-start.4 = (s32[16]{0:T(128)S(1)}, s32[16]{0:T(128)}, u32[]{:S(2)}) copy-start(s32[16]{0:T(128)} %param.11) | copy-start | bytes 196
  10.6 119.5 %all-gather.6.cloned.1.call-start = ((), (), s32[]{:S(2)}) async-start(), calls=%async_computation.3 | async-start | bytes 4718592 | tf_op jit(solution)/shard_map/all_gather | solution.py:51
  13.8 72.4 %all-to-all-start = ((bf16[8,512,2,128]{3,2,1,0:T(2,128)(2,1)}), bf16[8,512,2,128]{3,2,1,0:T(2,128)(2,1)S(1)}, u32[]{:S(2)}, u32[]{:S(2)}) async-start(bf16[8,512,2,128]{3,2,1,0:T(2,128)(2,1)} %stack.6), calls=%async_computation | async-start | bytes 4194304 | tf_op jit(solution)/shard_map/all_to_all | solution.py:53
  21.1 191.9 %all-gather.8.cloned.1.call-start = ((), (), s32[]{:S(2)}) async-start(), calls=%async_computation.4 | async-start | bytes 4718592 | tf_op jit(solution)/shard_map/all_gather | solution.py:126
  21.8 242.8 %reduce-scatter.2.cloned.1.call-start = ((), (), s32[]{:S(2)}) async-start(), calls=%async_computation.5 | async-start | bytes 5242880 | tf_op jit(solution)/shard_map/reduce_scatter | solution.py:127
  89.6 0.8 copy-start
  137.4 2.3 copy-start.1
  139.7 1.6 copy-start.3
  141.5 9.2 %collective-permute-start = (bf16[512,2,1,128]{3,0,2,1:T(8,128)(2,1)S(1)}, bf16[512,2,1,128]{3,0,2,1:T(8,128)(2,1)S(1)}, u32[]{:S(2)}, u32[]{:S(2)}) collective-permute-start(bf16[512,2,1,128]{3,0,2,1:T(8,128)(2,1)S(1)} %get-tuple-element.421), channel_id=1, source_target_pairs={{0,1},{1,2},{2,3},{3,4},{4,5},{5,6},{6,7},{8,9},{9,10},{10,11},{11... | collective-permute-start | bytes 786440 | tf_op jit(solution)/shard_map/while/body/eval_jaxpr/ppermute | solution.py:15
  154.6 12.5 %collective-permute-start = (bf16[512,2,1,128]{3,0,2,1:T(8,128)(2,1)S(1)}, bf16[512,2,1,128]{3,0,2,1:T(8,128)(2,1)S(1)}, u32[]{:S(2)}, u32[]{:S(2)}) collective-permute-start(bf16[512,2,1,128]{3,0,2,1:T(8,128)(2,1)S(1)} %get-tuple-element.421), channel_id=1, source_target_pairs={{0,1},{1,2},{2,3},{3,4},{4,5},{5,6},{6,7},{8,9},{9,10},{10,11},{11... | collective-permute-start | bytes 786440 | tf_op jit(solution)/shard_map/while/body/eval_jaxpr/ppermute | solution.py:15
Sparse Core Ops, SparseCore 0:
  10.7 37.1 all-gather.3
  50.1 80.0 all-gather.5
  132.3 80.6 all-gather.7
  219.6 44.9 reduce-scatter.1
